TPU v7x, 32 devices: a 4x4x1 block of a 4x4x8 slice. The times are simulated.
32 devices in a mesh: dp: 1 (over z), ep: 32 (over y, x, core).
Axes of the slice: x: 4, y: 4, z: 1, core: 2. Of those that a mesh axis runs over, the one named last changes fastest.
The devices are a block of a 4x4x8 slice.
Arguments:
- tokens: bfloat16 [131072, 1024], P(('dp', 'ep'))
- choice_idx: int32 [32, 8192], P(('dp', 'ep'))
- gate_weight: float32 [32, 8192], P(('dp', 'ep'))
- w_in: bfloat16 [32, 1024, 4096], P('ep')
- w_out: bfloat16 [32, 4096, 1024], P('ep')
Outputs:
- output: bfloat16 [131072, 1024], P(('dp', 'ep'))
All inputs are finite; a program needn't handle non-finite values.
Results may differ from a plain program's by a relative error of at most 0.00637701.
Values are sent between devices in bfloat16 or wider.
A program may use at most 768 MiB of HBM per device.

v0:
```python
import jax
import jax.numpy as jnp
from jax import lax
from jax.sharding import PartitionSpec as P


def solution(mesh):
    group_n = mesh.shape["ep"]
    row_spec = P(("dp", "ep"), None)
    expert_spec = P("ep", None, None)

    def local_layer(tok_loc, sel_loc, gate_loc, win_loc, wout_loc):
        tok_count, model_dim = tok_loc.shape
        exp_count, cap_slots = sel_loc.shape
        slot_total = exp_count * cap_slots
        pair_cap = 2 * slot_total // group_n
        flat_sel = sel_loc.reshape(slot_total)
        src_dev = flat_sel // tok_count
        src_row = flat_sel % tok_count
        slot_order = jnp.argsort(src_dev, stable=True)
        counts = jax.ops.segment_sum(jnp.ones_like(src_dev), src_dev, num_segments=group_n)
        starts = jnp.cumsum(counts) - counts
        lane_idx = jnp.arange(pair_cap, dtype=jnp.int32)
        is_valid = lane_idx[None, :] < counts[:, None]
        slot_of = slot_order[jnp.minimum(starts[:, None] + lane_idx[None, :], slot_total - 1)]
        request = jnp.where(is_valid, src_row[slot_of], 0)
        sorted_rank = jnp.zeros(slot_total, jnp.int32).at[slot_order].set(jnp.arange(slot_total, dtype=jnp.int32))
        recv_place = src_dev * pair_cap + sorted_rank - starts[src_dev]
        asked_rows = lax.all_to_all(request, "ep", 0, 0, tiled=True)
        send_rows = tok_loc[asked_rows]
        got_rows = lax.all_to_all(send_rows, "ep", 0, 0, tiled=True)
        expert_in = got_rows.reshape(group_n * pair_cap, model_dim)[recv_place].reshape(exp_count, cap_slots, model_dim)
        pre_act = jnp.einsum("ecd,edf->ecf", expert_in, win_loc, preferred_element_type=jnp.float32)
        hidden = jax.nn.gelu(pre_act, approximate=True).astype(jnp.bfloat16)
        expert_out = jnp.einsum("ecf,efd->ecd", hidden, wout_loc, preferred_element_type=jnp.float32)
        weighted = (gate_loc[:, :, None] * expert_out).astype(jnp.bfloat16).reshape(slot_total, model_dim)
        back_rows = jnp.where(is_valid[:, :, None], weighted[slot_of], jnp.zeros((), jnp.bfloat16))
        returned = lax.all_to_all(back_rows, "ep", 0, 0, tiled=True)
        added = jax.ops.segment_sum(returned.reshape(group_n * pair_cap, model_dim).astype(jnp.float32), asked_rows.reshape(group_n * pair_cap), num_segments=tok_count)
        return (tok_loc.astype(jnp.float32) + added).astype(jnp.bfloat16)

    return jax.shard_map(local_layer, mesh=mesh, in_specs=(row_spec, row_spec, row_spec, expert_spec, expert_spec), out_specs=row_spec, check_vma=False)
```

profile of v0, /device:TPU:107, one launch (start us, length us, event | category | flops | bytes accessed | tf_op | source)
XLA Modules:
  0.0 1863.4 jit_solution(2275466365696040233)
XLA Ops:
  0.0 0.9 and_select_fusion
  0.9 57.0 %scatter_custom_fusion = s32[32]{0:T(128)S(1)} fusion(s32[8192]{0:T(1024)S(1)} %bitcast.79, s32[8192]{0:T(1024)S(1)} %broadcast.298, s32[]{:T(128)} %constant.18.clone.1), kind=kCustom, calls=%fused_computation.82 | custom fusion | flops 8192 | bytes 132 | tf_op jit(solution)/shard_map/scatter-add | solution.py:21
  57.9 0.1 copy.7
  58.1 0.1 reduce
  58.2 0.8 add_select_fusion
  59.0 0.2 compare_select_fusion.2
  59.2 6.8 sort.17
  66.0 90.5 %gather_fusion = s32[16384]{0:T(1024)S(1)} fusion(s32[8192]{0:T(1024)S(1)} %get-tuple-element.6, s32[16384]{0:T(1024)S(1)} %broadcast_clamp_fusion.1), kind=kCustom, calls=%fused_computation | custom fusion | bytes 196608 | tf_op jit(solution)/shard_map/gather | solution.py:25
  156.6 90.5 %gather_fusion.1 = s32[16384]{0:T(1024)S(1)} fusion(s32[8192]{0:T(1024)S(1)} %get-tuple-element.35, s32[16384]{0:T(1024)S(1)} %broadcast_clamp_fusion.2), kind=kCustom, calls=%fused_computation.1 | custom fusion | bytes 196608 | tf_op jit(solution)/shard_map/gather | solution.py:26
  247.2 0.1 compare_select_fusion.3
  247.3 12.9 all_to_all.19
  260.3 0.6 copy-done.3
  260.9 84.5 %gather_fusion.2 = bf16[16384,1024]{1,0:T(8,128)(2,1)} fusion(bf16[4096,1024]{1,0:T(8,128)(2,1)} %param.5, s32[16384]{0:T(1024)S(1)} %broadcast_clamp_fusion), kind=kCustom, calls=%fused_computation.2 | custom fusion | bytes 67174400 | tf_op jit(solution)/shard_map/gather | solution.py:30
  345.4 6.5 all-to-all-start.1
  352.0 42.2 %scatter_custom_fusion.1 = s32[8192]{0:T(1024)S(1)} fusion(s32[8192]{0:T(1024)S(1)} %compare_select_fusion.12, s32[8192]{0:T(1024)S(1)} %iota.21, s32[]{:T(128)} %constant.18.clone.1), kind=kCustom, calls=%fused_computation.80 | custom fusion | bytes 32772 | tf_op jit(solution)/shard_map/scatter | solution.py:27
  394.2 0.7 fusion.20
  394.9 0.7 fusion.19
  395.6 4.7 compare_select_fusion.5
  400.3 2.5 compare_reduce_fusion.24
  402.8 0.7 iota_compare_fusion
  403.5 15.8 fusion.12
  419.2 388.3 %all-to-all-done.1 = bf16[32,512,1024]{2,1,0:T(8,128)(2,1)} async-done(((bf16[32,512,1024]{2,1,0:T(8,128)(2,1)}), bf16[32,512,1024]{2,1,0:T(8,128)(2,1)}, u32[]{:S(2)}, u32[]{:S(2)}) %all-to-all-start.1) | async-done | bytes 33554464 | tf_op jit(solution)/shard_map/all_to_all | solution.py:31
  807.6 150.5 %gather_fusion.3 = bf16[8192,1024]{1,0:T(8,128)(2,1)} fusion(bf16[16384,1024]{1,0:T(8,128)(2,1)} %bitcast.13, s32[8192]{0:T(1024)S(1)} %fusion.12), kind=kCustom, calls=%fused_computation.3 | custom fusion | bytes 33587200 | tf_op jit(solution)/shard_map/gather | solution.py:32
  958.1 101.7 %fusion.7 = bf16[8192,4096]{1,0:T(8,128)(2,1)} fusion(bf16[8192,1024]{1,0:T(8,128)(2,1)} %gather_fusion.3, bf16[1,1024,4096]{2,1,0:T(8,128)(2,1)} %param.8), kind=kOutput, calls=%fused_computation.16 | convolution fusion | flops 69021466624 | bytes 92274688 | tf_op jit(solution)/shard_map/ecd,edf->ecf/dot_general | solution.py:33
  1059.9 77.6 %multiply_convert_fusion = bf16[8192,1024]{1,0:T(8,128)(2,1)} fusion(bf16[8192,4096]{1,0:T(8,128)(2,1)} %fusion.7, f32[8192]{0:T(1024)S(1)} %bitcast.81, bf16[1,4096,1024]{2,1,0:T(8,128)(2,1)} %param.9), kind=kOutput, calls=%fused_computation.19 | convolution fusion | flops 68736253952 | bytes 92307456 | tf_op jit(solution)/shard_map/ecf,efd->ecd/dot_general | solution.py:35
  1137.5 88.1 %gather_fusion.4 = bf16[16384,1024]{1,0:T(8,128)(2,1)} fusion(bf16[8192,1024]{1,0:T(8,128)(2,1)} %multiply_convert_fusion, s32[16384]{0:T(1024)S(1)} %copy-done.1), kind=kCustom, calls=%fused_computation.4 | custom fusion | bytes 67174400 | tf_op jit(solution)/shard_map/gather | solution.py:37
  1225.6 22.8 %broadcast_select_fusion = bf16[32,512,1024]{2,1,0:T(8,128)(2,1)} fusion(bf16[32,512,1024]{2,1,0:T(8,128)(2,1)} %bitcast.68, pred[32,512]{1,0:T(8,128)(4,1)S(1)} %copy-done.4), kind=kLoop, calls=%fused_computation.20 | loop fusion | flops 16777216 | bytes 67125248 | tf_op jit(solution)/shard_map/jit(_where)/select_n | solution.py:37
  1248.4 4.7 all-to-all-start.2
  1253.1 11.3 convert_element_type.20
  1264.5 442.2 %all-to-all-done.2 = bf16[32,512,1024]{2,1,0:T(8,128)(2,1)} async-done(((bf16[32,512,1024]{2,1,0:T(8,128)(2,1)}), bf16[32,512,1024]{2,1,0:T(8,128)(2,1)}, u32[]{:S(2)}, u32[]{:S(2)}) %all-to-all-start.2) | async-done | bytes 33554464 | tf_op jit(solution)/shard_map/all_to_all | solution.py:38
  1706.6 147.2 %scatter_custom_fusion.2 = f32[4096,1024]{1,0:T(8,128)} fusion(f32[4096,1024]{1,0:T(8,128)} %convert_element_type.20, s32[16384]{0:T(1024)} %bitcast.72, bf16[16384,1024]{1,0:T(8,128)(2,1)} %bitcast.51), kind=kCustom, calls=%fused_computation.17 | custom fusion | flops 33554432 | bytes 50331648 | tf_op jit(solution)/shard_map/scatter-add | solution.py:39
  1853.9 9.1 convert_element_type.25
  (22 shorter events, 0.3 us)
Async XLA Ops:
  156.6 90.6 %copy-start = (s32[16384]{0:T(1024)}, s32[16384]{0:T(1024)S(1)}, u32[]{:S(2)}) copy-start(s32[16384]{0:T(1024)S(1)} %broadcast_clamp_fusion.2) | copy-start | bytes 196612
  260.2 0.6 copy-start.3
  345.4 50.2 %copy-start.2 = (s32[1,8192]{1,0:T(1,128)S(1)}, s32[1,8192]{1,0:T(1,128)}, u32[]{:S(2)}) copy-start(s32[1,8192]{1,0:T(1,128)} %param.6) | copy-start | bytes 98308
  345.4 462.2 %all-to-all-start.1 = ((bf16[32,512,1024]{2,1,0:T(8,128)(2,1)}), bf16[32,512,1024]{2,1,0:T(8,128)(2,1)}, u32[]{:S(2)}, u32[]{:S(2)}) async-start(bf16[32,512,1024]{2,1,0:T(8,128)(2,1)} %bitcast.69), calls=%async_computation.1 | async-start | bytes 67108864 | tf_op jit(solution)/shard_map/all_to_all | solution.py:31
  958.1 101.7 %copy-start.5 = (f32[1,8192]{1,0:T(1,128)S(1)}, f32[1,8192]{1,0:T(1,128)}, u32[]{:S(2)}) copy-start(f32[1,8192]{1,0:T(1,128)} %param.7) | copy-start | bytes 98308
  1059.8 77.6 %copy-start.1 = (s32[16384]{0:T(1024)S(1)}, s32[16384]{0:T(1024)}, u32[]{:S(2)}) copy-start(s32[16384]{0:T(1024)} %copy-done) | copy-start | bytes 196612
  1137.5 88.1 %copy-start.4 = (pred[32,512]{1,0:T(8,128)(4,1)S(1)}, pred[32,512]{1,0:T(8,128)(4,1)}, u32[]{:S(2)}) copy-start(pred[32,512]{1,0:T(8,128)(4,1)} %iota_compare_fusion) | copy-start | bytes 49156
  1248.4 458.2 %all-to-all-start.2 = ((bf16[32,512,1024]{2,1,0:T(8,128)(2,1)}), bf16[32,512,1024]{2,1,0:T(8,128)(2,1)}, u32[]{:S(2)}, u32[]{:S(2)}) async-start(bf16[32,512,1024]{2,1,0:T(8,128)(2,1)} %broadcast_select_fusion), calls=%async_computation.2 | async-start | bytes 67108864 | tf_op jit(solution)/shard_map/all_to_all | solution.py:38
where the time goes:
time: 1870 us; the launch traced here: 1860 us
  waiting for transfers between devices  831 us (44%)
  local copies, waits for them, and re-layouts  549 us (29%)
  other arithmetic  280 us (15%)
  matrix products  179 us (10%)
    all_to_all x1, waiting for transfers between devices, local_layer(): returned = lax.all_to_all(back_rows, 'ep', 0, 0, tiled=True)  442 us
    all_to_all x1, waiting for transfers between devices, local_layer(): got_rows = lax.all_to_all(send_rows, 'ep', 0, 0, tiled=True)  388 us
    gather x1, local copies, waits for them, and re-layouts, local_layer(): got_rows.reshape(group_n * pair_cap, model_dim)[recv_place]  151 us
    scatter-add x1, other arithmetic, local_layer(): jax.ops.segment_sum(returned.reshape(group_n * pair_cap, model_dim).astyp...  147 us
    dot_general x1, matrix products, local_layer(): jnp.einsum('ecd,edf->ecf', expert_in, win_loc, preferred_element_type=jnp...  102 us
    gather x1, local copies, waits for them, and re-layouts, local_layer(): request = jnp.where(is_valid, src_row[slot_of], 0)  90.5 us
    gather x1, local copies, waits for them, and re-layouts, local_layer(): slot_order[jnp.minimum(starts[:, None] + lane_idx[None, :], slot_total - 1)]  90.5 us
    gather x1, local copies, waits for them, and re-layouts, local_layer(): weighted[slot_of]  88.1 us
  transfers between devices with their start and end apart: 2, of which 2 were waited for; matrix products, arithmetic and copies ran while one was open for 4% of the time, Pallas kernels for 0%

commit v1 on v0

v1 whole, which is shorter than its diff:
```python
import jax
import jax.numpy as jnp
from jax import lax
from jax.experimental import pallas as pl
from jax.experimental.pallas import tpu as pltpu
from jax.sharding import PartitionSpec as P


def _windows(starts, sel, gate, group_n, width):
    tall = width // 128

    def body(st_ref, sel_ref, gate_ref, osel_ref, ogate_ref):
        def step(s, carry):
            st = st_ref[s]
            row = st // 128
            off = st % 128
            lane = lax.broadcasted_iota(jnp.int32, (8, 128), 1)
            for src, dst in ((sel_ref, osel_ref), (gate_ref, ogate_ref)):
                blk = src[pl.ds(row, 8), :]
                y = pltpu.roll(blk, lax.rem(128 - off, 128), 1)
                z = pltpu.roll(y, 7, 0)
                dst[s] = jnp.where(lane < 128 - off, y, z)[:tall]
            return carry

        lax.fori_loop(0, group_n, step, 0)

    n = sel.shape[0]
    pad = 8 * 128
    sel2 = jnp.pad(sel, (0, pad)).reshape(-1, 128)
    gate2 = jnp.pad(gate, (0, pad)).reshape(-1, 128)
    return pl.pallas_call(
        body,
        grid_spec=pltpu.PrefetchScalarGridSpec(
            num_scalar_prefetch=1,
            grid=(),
            in_specs=[pl.BlockSpec(memory_space=pltpu.VMEM)] * 2,
            out_specs=[pl.BlockSpec(memory_space=pltpu.VMEM)] * 2,
        ),
        out_shape=[
            jax.ShapeDtypeStruct((group_n, tall, 128), jnp.int32),
            jax.ShapeDtypeStruct((group_n, tall, 128), jnp.float32),
        ],
    )(starts, sel2, gate2)


def solution(mesh):
    group_n = mesh.shape["ep"]
    row_spec = P(("dp", "ep"), None)
    expert_spec = P("ep", None, None)

    def local_layer(tok_loc, sel_loc, gate_loc, win_loc, wout_loc):
        tok_count, model_dim = tok_loc.shape
        exp_count, cap_slots = sel_loc.shape
        n = exp_count * cap_slots
        pair_cap = 2 * n // group_n
        sel, gate = lax.sort((sel_loc.reshape(n), gate_loc.reshape(n)), num_keys=1)
        bounds = jnp.arange(group_n + 1, dtype=jnp.int32) * tok_count
        edges = jnp.sum((sel[None, :] < bounds[:, None]).astype(jnp.int32), axis=1)
        counts = edges[1:] - edges[:-1]
        wsel, wgate = _windows(edges[:-1], sel, gate, group_n, pair_cap)
        lane = jnp.arange(pair_cap, dtype=jnp.int32)
        request = jnp.where(lane[None] < counts[:, None], wsel.reshape(group_n, pair_cap) - bounds[:-1, None], -1)
        wgate = wgate.reshape(group_n, pair_cap)
        asked = lax.all_to_all(request, "ep", 0, 0, tiled=True)
        cuts = (0, pair_cap // 8, pair_cap * 9 // 16, pair_cap)
        parts = [slice(cuts[i], cuts[i + 1]) for i in range(3)]
        got = []
        for part in parts:
            idx = jnp.maximum(asked[:, part], 0).reshape(-1)
            rows = tok_loc[idx].reshape(group_n, part.stop - part.start, model_dim)
            got.append(lax.all_to_all(rows, "ep", 0, 0, tiled=True))
        weighted = []
        for part, x in zip(parts, got):
            pre = jnp.dot(x.reshape(-1, model_dim), win_loc[0], preferred_element_type=jnp.float32)
            hidden = jax.nn.gelu(pre, approximate=True).astype(jnp.bfloat16)
            o = jnp.dot(hidden, wout_loc[0], preferred_element_type=jnp.float32)
            g = wgate[:, part].reshape(-1)
            weighted.append((g[:, None] * o).astype(jnp.bfloat16).reshape(x.shape))

        def add_rows(acc, part, rows):
            idx = asked[:, part].reshape(-1)
            at = jnp.where(idx < 0, tok_count, idx)
            return acc.at[at].add(rows.reshape(-1, model_dim).astype(jnp.float32), mode="drop")

        acc = tok_loc.astype(jnp.float32)
        back1 = lax.all_to_all(weighted[1], "ep", 0, 0, tiled=True)
        back2 = lax.all_to_all(weighted[2], "ep", 0, 0, tiled=True)
        acc = add_rows(acc, parts[1], back1)
        last, acc, back2 = lax.optimization_barrier((weighted[0], acc, back2))
        back0 = lax.all_to_all(last, "ep", 0, 0, tiled=True)
        acc = add_rows(acc, parts[2], back2)
        acc = add_rows(acc, parts[0], back0)
        return acc.astype(jnp.bfloat16)

    return jax.shard_map(local_layer, mesh=mesh, in_specs=(row_spec, row_spec, row_spec, expert_spec, expert_spec), out_specs=row_spec, check_vma=False)
```

time: 1870 us -> 1040 us (0.56)
  the two profiles are of different devices: /device:TPU:107 before, /device:TPU:97 now
where the time goes in v1:
time: 1040 us; the launch traced here: 1030 us
  matrix products  365 us (35%)
  waiting for transfers between devices  236 us (23%)
  other arithmetic  204 us (20%)
  starting transfers between devices  102 us (10%)
  local copies, waits for them, and re-layouts  101 us (10%)
  blocking collectives  16.1 us (2%)
    dot_general x3, matrix products, local_layer(): jnp.dot(x.reshape(-1, model_dim), win_loc[0], preferred_element_type=jnp....  204 us
    scatter-add x3, other arithmetic, add_rows(): acc.at[at].add(rows.reshape(-1, model_dim).astype(jnp.float32), mode='drop')  173 us
    all_to_all x3, waiting for transfers between devices, local_layer(): got.append(lax.all_to_all(rows, 'ep', 0, 0, tiled=True))  170 us
    dot_general x3, matrix products, local_layer(): o = jnp.dot(hidden, wout_loc[0], preferred_element_type=jnp.float32)  161 us
    gather x3, local copies, waits for them, and re-layouts, local_layer(): rows = tok_loc[idx].reshape(group_n, part.stop - part.start, model_dim)  95.9 us
    all_to_all x1, waiting for transfers between devices, local_layer(): back2 = lax.all_to_all(weighted[2], 'ep', 0, 0, tiled=True)  45 us
    all_to_all x3, starting transfers between devices, local_layer(): got.append(lax.all_to_all(rows, 'ep', 0, 0, tiled=True))  36 us
    all_to_all x1, starting transfers between devices, local_layer(): back2 = lax.all_to_all(weighted[2], 'ep', 0, 0, tiled=True)  24.3 us
  transfers between devices with their start and end apart: 6, of which 5 were waited for; matrix products, arithmetic and copies ran while one was open for 59% of the time, Pallas kernels for 0%

profile of v1, /device:TPU:97, one launch (start us, length us, event | category | flops | bytes accessed | tf_op | source)
XLA Modules:
  0.0 1028.1 jit_solution(9124468767329546856)
XLA Ops:
  0.0 7.7 sort.23
  9.8 4.5 shard_map.55
  14.3 1.0 compare_select_fusion
  15.3 16.1 %all_to_all.39 = s32[32,1,512]{2,1,0:T(1,128)S(1)} all-to-all(s32[32,1,512]{2,1,0:T(1,128)S(1)} %compare_select_fusion), channel_id=1, replica_groups=mesh['dp'=1,'ep'=32] {'ep'}, dimensions={0} | all-to-all | bytes 131072 | tf_op jit(solution)/shard_map/all_to_all | solution.py:64
  32.2 15.4 %gather_fusion = bf16[2048,1024]{1,0:T(8,128)(2,1)} fusion(bf16[4096,1024]{1,0:T(8,128)(2,1)} %param.5, s32[2048]{0:T(1024)S(1)} %broadcast_clamp_fusion.2), kind=kCustom, calls=%fused_computation | custom fusion | bytes 8396800 | tf_op jit(solution)/shard_map/gather | solution.py:70
  47.6 3.8 all-to-all-start.1
  51.3 0.7 fusion.46
  52.2 40.3 %gather_fusion.1 = bf16[7168,1024]{1,0:T(8,128)(2,1)} fusion(bf16[4096,1024]{1,0:T(8,128)(2,1)} %param.5, s32[7168]{0:T(1024)S(1)} %broadcast_clamp_fusion.1), kind=kCustom, calls=%fused_computation.1 | custom fusion | bytes 29388800 | tf_op jit(solution)/shard_map/gather | solution.py:70
  92.5 10.1 all-to-all-done.1
  102.7 9.6 all-to-all-start.2
  113.0 0.7 mul.99
  114.5 40.2 %gather_fusion.2 = bf16[7168,1024]{1,0:T(8,128)(2,1)} fusion(bf16[4096,1024]{1,0:T(8,128)(2,1)} %param.5, s32[7168]{0:T(1024)S(1)} %broadcast_clamp_fusion), kind=kCustom, calls=%fused_computation.2 | custom fusion | bytes 29388800 | tf_op jit(solution)/shard_map/gather | solution.py:70
  154.8 136.8 %all-to-all-done.2 = bf16[32,224,1024]{2,1,0:T(8,128)(2,1)} async-done(((bf16[32,224,1024]{2,1,0:T(8,128)(2,1)}), bf16[32,224,1024]{2,1,0:T(8,128)(2,1)}, u32[]{:S(2)}, u32[]{:S(2)}) %all-to-all-start.2) | async-done | bytes 14680096 | tf_op jit(solution)/shard_map/all_to_all | solution.py:71
  291.6 22.6 %all-to-all-start.4 = ((bf16[32,224,1024]{2,1,0:T(8,128)(2,1)}), bf16[32,224,1024]{2,1,0:T(8,128)(2,1)}, u32[]{:S(2)}, u32[]{:S(2)}) async-start(bf16[32,224,1024]{2,1,0:T(8,128)(2,1)} %bitcast.68), calls=%async_computation.4 | async-start | bytes 29360128 | tf_op jit(solution)/shard_map/all_to_all | solution.py:71
  314.2 87.9 %fusion.7 = bf16[7168,4096]{1,0:T(8,128)(2,1)} fusion(bf16[7168,1024]{1,0:T(8,128)(2,1)} %bitcast.14, bf16[1,1024,4096]{2,1,0:T(8,128)(2,1)} %param.8), kind=kOutput, calls=%fused_computation.15 | convolution fusion | flops 60393783296 | bytes 81788928 | tf_op jit(solution)/shard_map/dot_general | solution.py:74
  402.1 69.0 %multiply_convert_fusion.1 = bf16[7168,1024]{1,0:T(8,128)(2,1)} fusion(bf16[7168,4096]{1,0:T(8,128)(2,1)} %fusion.7, f32[7168]{0:T(1024)S(1)} %copy-done.6, bf16[1,4096,1024]{2,1,0:T(8,128)(2,1)} %param.9), kind=kOutput, calls=%fused_computation.38 | convolution fusion | flops 60144222208 | bytes 81817600 | tf_op jit(solution)/shard_map/dot_general | solution.py:76
  471.1 23.2 %all-to-all-done.4 = bf16[32,224,1024]{2,1,0:T(8,128)(2,1)} async-done(((bf16[32,224,1024]{2,1,0:T(8,128)(2,1)}), bf16[32,224,1024]{2,1,0:T(8,128)(2,1)}, u32[]{:S(2)}, u32[]{:S(2)}) %all-to-all-start.4) | async-done | bytes 14680096 | tf_op jit(solution)/shard_map/all_to_all | solution.py:71
  494.3 19.5 %all-to-all-start.3 = ((bf16[32,224,1024]{2,1,0:T(8,128)(2,1)}), bf16[32,224,1024]{2,1,0:T(8,128)(2,1)}, u32[]{:S(2)}, u32[]{:S(2)}) async-start(bf16[32,224,1024]{2,1,0:T(8,128)(2,1)} %bitcast.71), calls=%async_computation.3 | async-start | bytes 29360128 | tf_op jit(solution)/shard_map/all_to_all | solution.py:86
  513.8 87.9 %fusion.15 = bf16[7168,4096]{1,0:T(8,128)(2,1)} fusion(bf16[7168,1024]{1,0:T(8,128)(2,1)} %bitcast.19, bf16[1,1024,4096]{2,1,0:T(8,128)(2,1)} %param.8), kind=kOutput, calls=%fused_computation.23 | convolution fusion | flops 60393783296 | bytes 81788928 | tf_op jit(solution)/shard_map/dot_general | solution.py:74
  601.7 69.2 %multiply_convert_fusion = bf16[7168,1024]{1,0:T(8,128)(2,1)} fusion(bf16[7168,4096]{1,0:T(8,128)(2,1)} %fusion.15, f32[7168]{0:T(1024)S(1)} %copy-done.5, bf16[1,4096,1024]{2,1,0:T(8,128)(2,1)} %param.9), kind=kOutput, calls=%fused_computation.37 | convolution fusion | flops 60144222208 | bytes 81817600 | tf_op jit(solution)/shard_map/dot_general | solution.py:76
  670.9 20.4 %all-to-all-done.3 = bf16[32,224,1024]{2,1,0:T(8,128)(2,1)} async-done(((bf16[32,224,1024]{2,1,0:T(8,128)(2,1)}), bf16[32,224,1024]{2,1,0:T(8,128)(2,1)}, u32[]{:S(2)}, u32[]{:S(2)}) %all-to-all-start.3) | async-done | bytes 14680096 | tf_op jit(solution)/shard_map/all_to_all | solution.py:86
  691.3 24.3 %all-to-all-start.5 = ((bf16[32,224,1024]{2,1,0:T(8,128)(2,1)}), bf16[32,224,1024]{2,1,0:T(8,128)(2,1)}, u32[]{:S(2)}, u32[]{:S(2)}) async-start(bf16[32,224,1024]{2,1,0:T(8,128)(2,1)} %bitcast.70), calls=%async_computation.5 | async-start | bytes 29360128 | tf_op jit(solution)/shard_map/all_to_all | solution.py:87
  715.7 11.3 %convert_element_type.50 = f32[4096,1024]{1,0:T(8,128)} convert(bf16[4096,1024]{1,0:T(8,128)(2,1)} %param.5) | non-fusion elementwise | flops 4194304 | bytes 25165824 | tf_op jit(solution)/shard_map/convert_element_type | solution.py:85
  726.9 0.7 slice.46
  727.9 28.2 %fusion.23.clone.4 = bf16[2048,4096]{1,0:T(8,128)(2,1)S(1)} fusion(bf16[2048,1024]{1,0:T(8,128)(2,1)} %bitcast.7, bf16[1,1024,4096]{2,1,0:T(8,128)(2,1)} %param.8), kind=kOutput, calls=%fused_computation.32.clone.clone.clone.1 | convolution fusion | flops 17255366656 | bytes 29360128 | tf_op jit(solution)/shard_map/dot_general | solution.py:74
  756.1 22.4 %multiply_convert_fusion.2 = bf16[2048,1024]{1,0:T(8,128)(2,1)} fusion(bf16[1,4096,1024]{2,1,0:T(8,128)(2,1)} %param.9, f32[2048]{0:T(1024)S(1)} %mul.89, bf16[2048,4096]{1,0:T(8,128)(2,1)S(1)} %fusion.23.clone.4), kind=kOutput, calls=%fused_computation.48 | convolution fusion | flops 17184063488 | bytes 29368320 | tf_op jit(solution)/shard_map/dot_general | solution.py:76
  778.5 71.7 %scatter_custom_fusion = f32[4096,1024]{1,0:T(8,128)} fusion(f32[4096,1024]{1,0:T(8,128)} %convert_element_type.50, s32[7168]{0:T(1024)S(1)} %bitcast.84, bf16[7168,1024]{1,0:T(8,128)(2,1)} %bitcast.25), kind=kCustom, calls=%fused_computation.35 | custom fusion | flops 14680064 | bytes 31457280 | tf_op jit(solution)/shard_map/scatter-add | solution.py:83
  850.1 45.0 %all-to-all-done.5 = bf16[32,224,1024]{2,1,0:T(8,128)(2,1)} async-done(((bf16[32,224,1024]{2,1,0:T(8,128)(2,1)}), bf16[32,224,1024]{2,1,0:T(8,128)(2,1)}, u32[]{:S(2)}, u32[]{:S(2)}) %all-to-all-start.5) | async-done | bytes 14680096 | tf_op jit(solution)/shard_map/all_to_all | solution.py:87
  895.2 22.4 %all-to-all-start.6 = ((bf16[32,64,1024]{2,1,0:T(8,128)(2,1)}), bf16[32,64,1024]{2,1,0:T(8,128)(2,1)}, u32[]{:S(2)}, u32[]{:S(2)}) async-start(bf16[32,64,1024]{2,1,0:T(8,128)(2,1)} %bitcast.72), calls=%async_computation.6 | async-start | bytes 8388608 | tf_op jit(solution)/shard_map/all_to_all | solution.py:90
  917.8 71.5 %scatter_custom_fusion.1 = f32[4096,1024]{1,0:T(8,128)} fusion(f32[4096,1024]{1,0:T(8,128)} %scatter_custom_fusion, s32[7168]{0:T(1024)S(1)} %bitcast.85, bf16[7168,1024]{1,0:T(8,128)(2,1)} %bitcast.26), kind=kCustom, calls=%fused_computation.33 | custom fusion | flops 14680064 | bytes 31457280 | tf_op jit(solution)/shard_map/scatter-add | solution.py:83
  989.4 29.5 %scatter_custom_fusion.2 = f32[4096,1024]{1,0:T(8,128)} fusion(f32[4096,1024]{1,0:T(8,128)} %scatter_custom_fusion.1, s32[2048]{0:T(1024)S(1)} %bitcast.86, bf16[2048,1024]{1,0:T(8,128)(2,1)} %bitcast.27), kind=kCustom, calls=%fused_computation.39 | custom fusion | flops 4194304 | bytes 20971520 | tf_op jit(solution)/shard_map/scatter-add | solution.py:83
  1018.9 9.1 convert_element_type.61
  (42 shorter events, 5.1 us)
Async XLA Ops:
  47.6 55.1 %all-to-all-start.1 = ((bf16[32,64,1024]{2,1,0:T(8,128)(2,1)}), bf16[32,64,1024]{2,1,0:T(8,128)(2,1)}, u32[]{:S(2)}, u32[]{:S(2)}) async-start(bf16[32,64,1024]{2,1,0:T(8,128)(2,1)} %bitcast.69), calls=%async_computation.1 | async-start | bytes 8388608 | tf_op jit(solution)/shard_map/all_to_all | solution.py:71
  92.5 19.7 %copy-start.4 = (f32[32,4,128]{2,1,0:T(4,128)S(1)}, f32[32,4,128]{2,1,0:T(4,128)}, u32[]{:S(2)}) copy-start(f32[32,4,128]{2,1,0:T(4,128)} %get-tuple-element.16) | copy-start | bytes 196612
  102.7 188.9 %all-to-all-start.2 = ((bf16[32,224,1024]{2,1,0:T(8,128)(2,1)}), bf16[32,224,1024]{2,1,0:T(8,128)(2,1)}, u32[]{:S(2)}, u32[]{:S(2)}) async-start(bf16[32,224,1024]{2,1,0:T(8,128)(2,1)} %bitcast.67), calls=%async_computation.2 | async-start | bytes 29360128 | tf_op jit(solution)/shard_map/all_to_all | solution.py:71
  112.3 0.6 copy-start
  291.6 202.7 %all-to-all-start.4 = ((bf16[32,224,1024]{2,1,0:T(8,128)(2,1)}), bf16[32,224,1024]{2,1,0:T(8,128)(2,1)}, u32[]{:S(2)}, u32[]{:S(2)}) async-start(bf16[32,224,1024]{2,1,0:T(8,128)(2,1)} %bitcast.68), calls=%async_computation.4 | async-start | bytes 29360128 | tf_op jit(solution)/shard_map/all_to_all | solution.py:71
  314.2 88.0 %copy-start.6 = (f32[7168]{0:T(1024)S(1)}, f32[7168]{0:T(1024)}, u32[]{:S(2)}) copy-start(f32[7168]{0:T(1024)} %mul.99) | copy-start | bytes 86020
  494.3 197.0 %all-to-all-start.3 = ((bf16[32,224,1024]{2,1,0:T(8,128)(2,1)}), bf16[32,224,1024]{2,1,0:T(8,128)(2,1)}, u32[]{:S(2)}, u32[]{:S(2)}) async-start(bf16[32,224,1024]{2,1,0:T(8,128)(2,1)} %bitcast.71), calls=%async_computation.3 | async-start | bytes 29360128 | tf_op jit(solution)/shard_map/all_to_all | solution.py:86
  513.8 87.9 %copy-start.5 = (f32[7168]{0:T(1024)S(1)}, f32[7168]{0:T(1024)}, u32[]{:S(2)}) copy-start(f32[7168]{0:T(1024)} %mul.106) | copy-start | bytes 86020
  691.3 203.8 %all-to-all-start.5 = ((bf16[32,224,1024]{2,1,0:T(8,128)(2,1)}), bf16[32,224,1024]{2,1,0:T(8,128)(2,1)}, u32[]{:S(2)}, u32[]{:S(2)}) async-start(bf16[32,224,1024]{2,1,0:T(8,128)(2,1)} %bitcast.70), calls=%async_computation.5 | async-start | bytes 29360128 | tf_op jit(solution)/shard_map/all_to_all | solution.py:87
  715.7 12.1 %copy-start.2 = (s32[32,224]{1,0:T(8,128)S(1)}, s32[32,224]{1,0:T(8,128)}, u32[]{:S(2)}) copy-start(s32[32,224]{1,0:T(8,128)} %get-tuple-element.26) | copy-start | bytes 86020
  778.5 139.1 %copy-start.1 = (s32[32,224]{1,0:T(8,128)S(1)}, s32[32,224]{1,0:T(8,128)}, u32[]{:S(2)}) copy-start(s32[32,224]{1,0:T(8,128)} %get-tuple-element.23) | copy-start | bytes 86020
  778.5 139.2 %copy-start.3 = (s32[32,64]{1,0:T(8,128)S(1)}, s32[32,64]{1,0:T(8,128)}, u32[]{:S(2)}) copy-start(s32[32,64]{1,0:T(8,128)} %get-tuple-element.21) | copy-start | bytes 24580
  895.2 94.2 %all-to-all-start.6 = ((bf16[32,64,1024]{2,1,0:T(8,128)(2,1)}), bf16[32,64,1024]{2,1,0:T(8,128)(2,1)}, u32[]{:S(2)}, u32[]{:S(2)}) async-start(bf16[32,64,1024]{2,1,0:T(8,128)(2,1)} %bitcast.72), calls=%async_computation.6 | async-start | bytes 8388608 | tf_op jit(solution)/shard_map/all_to_all | solution.py:90

commit v2 on v1

--- a/solution.py
+++ b/solution.py
@@ -62,12 +62,14 @@
         request = jnp.where(lane[None] < counts[:, None], wsel.reshape(group_n, pair_cap) - bounds[:-1, None], -1)
         wgate = wgate.reshape(group_n, pair_cap)
         asked = lax.all_to_all(request, "ep", 0, 0, tiled=True)
-        cuts = (0, pair_cap // 8, pair_cap * 9 // 16, pair_cap)
-        parts = [slice(cuts[i], cuts[i + 1]) for i in range(3)]
+        cuts = (0, pair_cap // 16, pair_cap * 3 // 16, pair_cap * 19 // 32, pair_cap)
+        parts = [slice(cuts[i], cuts[i + 1]) for i in range(4)]
         got = []
         for part in parts:
             idx = jnp.maximum(asked[:, part], 0).reshape(-1)
             rows = tok_loc[idx].reshape(group_n, part.stop - part.start, model_dim)
+            if got:
+                rows, got[-1] = lax.optimization_barrier((rows, got[-1]))
             got.append(lax.all_to_all(rows, "ep", 0, 0, tiled=True))
         weighted = []
         for part, x in zip(parts, got):
@@ -83,12 +85,15 @@
             return acc.at[at].add(rows.reshape(-1, model_dim).astype(jnp.float32), mode="drop")
 
         acc = tok_loc.astype(jnp.float32)
-        back1 = lax.all_to_all(weighted[1], "ep", 0, 0, tiled=True)
         back2 = lax.all_to_all(weighted[2], "ep", 0, 0, tiled=True)
+        back3 = lax.all_to_all(weighted[3], "ep", 0, 0, tiled=True)
+        acc = add_rows(acc, parts[2], back2)
+        short, weighted[0], acc, back3 = lax.optimization_barrier((weighted[1], weighted[0], acc, back3))
+        back1 = lax.all_to_all(short, "ep", 0, 0, tiled=True)
+        acc = add_rows(acc, parts[3], back3)
+        short, acc, back1 = lax.optimization_barrier((weighted[0], acc, back1))
+        back0 = lax.all_to_all(short, "ep", 0, 0, tiled=True)
         acc = add_rows(acc, parts[1], back1)
-        last, acc, back2 = lax.optimization_barrier((weighted[0], acc, back2))
-        back0 = lax.all_to_all(last, "ep", 0, 0, tiled=True)
-        acc = add_rows(acc, parts[2], back2)
         acc = add_rows(acc, parts[0], back0)
         return acc.astype(jnp.bfloat16)
 

time: 1040 us -> 1040 us (level)
  waiting for transfers between devices: 236 us -> 209 us
  other arithmetic: 204 us -> 218 us
    all_to_all x1, waiting for transfers between devices: 45 us -> 18.9 us  [local_layer(): back2 = lax.all_to_all(weighted[2], 'ep', 0, 0, tiled=True)]
    dot_general x3 -> x4, matrix products: 161 us -> 175 us  [local_layer(): o = jnp.dot(hidden, wout_loc[0], preferred_element_type=jnp.float32)]
    scatter-add x3 -> x4, other arithmetic: 173 us -> 185 us  [add_rows(): acc.at[at].add(rows.reshape(-1, model_dim).astype(jnp.float32), mode='drop')]
    all_to_all x2 -> x3, starting transfers between devices: 41.9 us -> 49.3 us  [the longest x1 21.5 us: local_layer(): back1 = lax.all_to_all(short, 'ep', 0, 0, tiled=True)]
    all_to_all x3 -> x4, waiting for transfers between devices: 170 us -> 166 us  [local_layer(): got.append(lax.all_to_all(rows, 'ep', 0, 0, tiled=True))]
    all_to_all x2 -> x3, waiting for transfers between devices: 20.4 us -> 23.6 us  [the longest x1 23.6 us: local_layer(): back3 = lax.all_to_all(weighted[3], 'ep', 0, 0, tiled=True)]
    gather x3 -> x4, local copies, waits for them, and re-layouts: 95.9 us -> 93.5 us  [local_layer(): rows = tok_loc[idx].reshape(group_n, part.stop - part.start, model_dim)]
    all_to_all x3 -> x4, starting transfers between devices: 36 us -> 38 us  [local_layer(): got.append(lax.all_to_all(rows, 'ep', 0, 0, tiled=True))]
  transfers between devices with their start and end apart: 6 -> 8, of which waited for: 5 -> 6; matrix products, arithmetic and copies ran while one was open for 59% -> 62% of each run, Pallas kernels for 0% -> 0%
where the time goes in v2:
time: 1040 us; the launch traced here: 1030 us
  matrix products  374 us (36%)
  other arithmetic  218 us (21%)
  waiting for transfers between devices  209 us (20%)
  starting transfers between devices  109 us (10%)
  local copies, waits for them, and re-layouts  98.4 us (9%)
  blocking collectives  16.1 us (2%)
    dot_general x3, matrix products, local_layer(): jnp.dot(x.reshape(-1, model_dim), win_loc[0], preferred_element_type=jnp....  199 us
    scatter-add x4, other arithmetic, add_rows(): acc.at[at].add(rows.reshape(-1, model_dim).astype(jnp.float32), mode='drop')  185 us
    dot_general x4, matrix products, local_layer(): o = jnp.dot(hidden, wout_loc[0], preferred_element_type=jnp.float32)  175 us
    all_to_all x4, waiting for transfers between devices, local_layer(): got.append(lax.all_to_all(rows, 'ep', 0, 0, tiled=True))  166 us
    gather x4, local copies, waits for them, and re-layouts, local_layer(): rows = tok_loc[idx].reshape(group_n, part.stop - part.start, model_dim)  93.5 us
    all_to_all x4, starting transfers between devices, local_layer(): got.append(lax.all_to_all(rows, 'ep', 0, 0, tiled=True))  38 us
    all_to_all x1, waiting for transfers between devices, local_layer(): back3 = lax.all_to_all(weighted[3], 'ep', 0, 0, tiled=True)  23.6 us
    all_to_all x1, starting transfers between devices, local_layer(): back1 = lax.all_to_all(short, 'ep', 0, 0, tiled=True)  21.5 us
  transfers between devices with their start and end apart: 8, of which 6 were waited for; matrix products, arithmetic and copies ran while one was open for 62% of the time, Pallas kernels for 0%

profile of v2, /device:TPU:97, one launch (start us, length us, event | category | flops | bytes accessed | tf_op | source)
XLA Modules:
  0.0 1029.5 jit_solution(12942826872381614569)
XLA Ops:
  0.0 7.7 sort.23
  15.2 16.1 %all_to_all.49 = s32[32,1,512]{2,1,0:T(1,128)S(1)} all-to-all(s32[32,1,512]{2,1,0:T(1,128)S(1)} %compare_select_fusion), channel_id=1, replica_groups=mesh['dp'=1,'ep'=32] {'ep'}, dimensions={0} | all-to-all | bytes 131072 | tf_op jit(solution)/shard_map/all_to_all | solution.py:64
  32.1 10.5 %gather_fusion.2 = bf16[1024,1024]{1,0:T(8,128)(2,1)} fusion(bf16[4096,1024]{1,0:T(8,128)(2,1)} %param.5, s32[1024]{0:T(1024)S(1)} %broadcast_clamp_fusion.1), kind=kCustom, calls=%fused_computation.2 | custom fusion | bytes 4198400 | tf_op jit(solution)/shard_map/gather | solution.py:70
  46.4 15.4 %gather_fusion.1 = bf16[2048,1024]{1,0:T(8,128)(2,1)} fusion(bf16[4096,1024]{1,0:T(8,128)(2,1)} %param.5, s32[2048]{0:T(1024)S(1)} %broadcast_clamp_fusion), kind=kCustom, calls=%fused_computation.1 | custom fusion | bytes 8396800 | tf_op jit(solution)/shard_map/gather | solution.py:70
  61.8 11.9 %all-to-all-done.1 = bf16[32,32,1024]{2,1,0:T(8,128)(2,1)S(1)} async-done(((bf16[32,32,1024]{2,1,0:T(8,128)(2,1)}), bf16[32,32,1024]{2,1,0:T(8,128)(2,1)S(1)}, u32[]{:S(2)}, u32[]{:S(2)}) %all-to-all-start.1) | async-done | bytes 2097184 | tf_op jit(solution)/shard_map/all_to_all | solution.py:73
  73.7 5.9 all-to-all-start.2
  80.5 33.8 %gather_fusion = bf16[6656,1024]{1,0:T(8,128)(2,1)} fusion(bf16[4096,1024]{1,0:T(8,128)(2,1)} %param.5, s32[7168]{0:T(1024)S(1)} %pad_clamp_fusion.1), kind=kCustom, calls=%fused_computation | custom fusion | bytes 27289600 | tf_op jit(solution)/shard_map/gather | solution.py:70
  114.3 16.7 %all-to-all-done.2 = bf16[32,64,1024]{2,1,0:T(8,128)(2,1)} async-done(((bf16[32,64,1024]{2,1,0:T(8,128)(2,1)}), bf16[32,64,1024]{2,1,0:T(8,128)(2,1)}, u32[]{:S(2)}, u32[]{:S(2)}) %all-to-all-start.2) | async-done | bytes 4194336 | tf_op jit(solution)/shard_map/all_to_all | solution.py:73
  131.0 10.1 all-to-all-start.3
  141.1 11.3 %convert_element_type.64 = f32[4096,1024]{1,0:T(8,128)} convert(bf16[4096,1024]{1,0:T(8,128)(2,1)} %param.5) | non-fusion elementwise | flops 4194304 | bytes 25165824 | tf_op jit(solution)/shard_map/convert_element_type | solution.py:87
  155.6 33.8 %gather_fusion.3 = bf16[6656,1024]{1,0:T(8,128)(2,1)} fusion(bf16[4096,1024]{1,0:T(8,128)(2,1)} %param.5, s32[7168]{0:T(1024)S(1)} %pad_clamp_fusion), kind=kCustom, calls=%fused_computation.3 | custom fusion | bytes 27289600 | tf_op jit(solution)/shard_map/gather | solution.py:70
  190.2 118.5 %all-to-all-done.3 = bf16[32,208,1024]{2,1,0:T(8,128)(2,1)} async-done(((bf16[32,208,1024]{2,1,0:T(8,128)(2,1)}), bf16[32,208,1024]{2,1,0:T(8,128)(2,1)}, u32[]{:S(2)}, u32[]{:S(2)}) %all-to-all-start.3) | async-done | bytes 13631520 | tf_op jit(solution)/shard_map/all_to_all | solution.py:73
  308.7 18.9 %all-to-all-start.5 = ((bf16[32,208,1024]{2,1,0:T(8,128)(2,1)}), bf16[32,208,1024]{2,1,0:T(8,128)(2,1)}, u32[]{:S(2)}, u32[]{:S(2)}) async-start(bf16[32,208,1024]{2,1,0:T(8,128)(2,1)} %bitcast.82), calls=%async_computation.5 | async-start | bytes 27262976 | tf_op jit(solution)/shard_map/all_to_all | solution.py:73
  327.6 84.2 %fusion.7 = bf16[6656,4096]{1,0:T(8,128)(2,1)} fusion(bf16[6656,1024]{1,0:T(8,128)(2,1)} %bitcast.17, bf16[1,1024,4096]{2,1,0:T(8,128)(2,1)} %param.8), kind=kOutput, calls=%fused_computation.17 | convolution fusion | flops 56079941632 | bytes 76546048 | tf_op jit(solution)/shard_map/dot_general | solution.py:76
  411.9 64.5 %multiply_convert_fusion.1 = bf16[6656,1024]{1,0:T(8,128)(2,1)} fusion(bf16[6656,4096]{1,0:T(8,128)(2,1)} %fusion.7, f32[6656]{0:T(1024)S(1)} %copy-done.7, bf16[1,4096,1024]{2,1,0:T(8,128)(2,1)} %param.9), kind=kOutput, calls=%fused_computation.40 | convolution fusion | flops 55848206336 | bytes 76572672 | tf_op jit(solution)/shard_map/dot_general | solution.py:78
  476.3 19.2 %all-to-all-done.5 = bf16[32,208,1024]{2,1,0:T(8,128)(2,1)} async-done(((bf16[32,208,1024]{2,1,0:T(8,128)(2,1)}), bf16[32,208,1024]{2,1,0:T(8,128)(2,1)}, u32[]{:S(2)}, u32[]{:S(2)}) %all-to-all-start.5) | async-done | bytes 13631520 | tf_op jit(solution)/shard_map/all_to_all | solution.py:73
  495.5 21.4 %all-to-all-start.4 = ((bf16[32,208,1024]{2,1,0:T(8,128)(2,1)}), bf16[32,208,1024]{2,1,0:T(8,128)(2,1)}, u32[]{:S(2)}, u32[]{:S(2)}) async-start(bf16[32,208,1024]{2,1,0:T(8,128)(2,1)} %bitcast.85), calls=%async_computation.4 | async-start | bytes 27262976 | tf_op jit(solution)/shard_map/all_to_all | solution.py:88
  516.9 84.4 %fusion.15 = bf16[6656,4096]{1,0:T(8,128)(2,1)} fusion(bf16[6656,1024]{1,0:T(8,128)(2,1)} %bitcast.20, bf16[1,1024,4096]{2,1,0:T(8,128)(2,1)} %param.8), kind=kOutput, calls=%fused_computation.25 | convolution fusion | flops 56079941632 | bytes 76546048 | tf_op jit(solution)/shard_map/dot_general | solution.py:76
  601.3 64.5 %multiply_convert_fusion = bf16[6656,1024]{1,0:T(8,128)(2,1)} fusion(bf16[6656,4096]{1,0:T(8,128)(2,1)} %fusion.15, f32[6656]{0:T(1024)S(1)} %copy-done.6, bf16[1,4096,1024]{2,1,0:T(8,128)(2,1)} %param.9), kind=kOutput, calls=%fused_computation.39 | convolution fusion | flops 55848206336 | bytes 76572672 | tf_op jit(solution)/shard_map/dot_general | solution.py:78
  665.8 18.9 %all-to-all-done.4 = bf16[32,208,1024]{2,1,0:T(8,128)(2,1)} async-done(((bf16[32,208,1024]{2,1,0:T(8,128)(2,1)}), bf16[32,208,1024]{2,1,0:T(8,128)(2,1)}, u32[]{:S(2)}, u32[]{:S(2)}) %all-to-all-start.4) | async-done | bytes 13631520 | tf_op jit(solution)/shard_map/all_to_all | solution.py:88
  684.7 21.5 %all-to-all-start.6 = ((bf16[32,208,1024]{2,1,0:T(8,128)(2,1)}), bf16[32,208,1024]{2,1,0:T(8,128)(2,1)}, u32[]{:S(2)}, u32[]{:S(2)}) async-start(bf16[32,208,1024]{2,1,0:T(8,128)(2,1)} %bitcast.84), calls=%async_computation.6 | async-start | bytes 27262976 | tf_op jit(solution)/shard_map/all_to_all | solution.py:89
  706.2 24.9 %multiply_convert_fusion.3 = bf16[1024,1024]{1,0:T(8,128)(2,1)} fusion(bf16[1,4096,1024]{2,1,0:T(8,128)(2,1)} %param.9, f32[1024]{0:T(1024)S(1)} %copy-done.9, bf16[1024,1024]{1,0:T(8,128)(2,1)S(1)} %bitcast.88, bf16[1,1024,4096]{2,1,0:T(8,128)(2,1)} %param.8), kind=kOutput, calls=%fused_computation.69 | convolution fusion | flops 17219715072 | bytes 20975616 | tf_op jit(solution)/shard_map/dot_general | solution.py:78
  731.1 30.6 %fusion.23.clone.4 = bf16[2048,4096]{1,0:T(8,128)(2,1)} fusion(bf16[2048,1024]{1,0:T(8,128)(2,1)} %bitcast.10, bf16[1,1024,4096]{2,1,0:T(8,128)(2,1)} %param.8), kind=kOutput, calls=%fused_computation.34.clone.clone.clone.1 | convolution fusion | flops 17255366656 | bytes 29360128 | tf_op jit(solution)/shard_map/dot_general | solution.py:76
  761.7 21.2 %multiply_convert_fusion.2 = bf16[2048,1024]{1,0:T(8,128)(2,1)} fusion(bf16[1,4096,1024]{2,1,0:T(8,128)(2,1)S(1)} %copy-done.10, f32[2048]{0:T(1024)S(1)} %copy-done.8, bf16[2048,4096]{1,0:T(8,128)(2,1)} %fusion.23.clone.4), kind=kOutput, calls=%fused_computation.66 | convolution fusion | flops 17184063488 | bytes 29368320 | tf_op jit(solution)/shard_map/dot_general | solution.py:78
  782.9 67.6 %scatter_custom_fusion = f32[4096,1024]{1,0:T(8,128)} fusion(f32[4096,1024]{1,0:T(8,128)} %convert_element_type.64, s32[6656]{0:T(1024)} %fusion.64, bf16[6656,1024]{1,0:T(8,128)(2,1)} %bitcast.27), kind=kCustom, calls=%fused_computation.37 | custom fusion | flops 13631488 | bytes 30408704 | tf_op jit(solution)/shard_map/scatter-add | solution.py:85
  850.5 23.6 %all-to-all-done.6 = bf16[32,208,1024]{2,1,0:T(8,128)(2,1)} async-done(((bf16[32,208,1024]{2,1,0:T(8,128)(2,1)}), bf16[32,208,1024]{2,1,0:T(8,128)(2,1)}, u32[]{:S(2)}, u32[]{:S(2)}) %all-to-all-start.6) | async-done | bytes 13631520 | tf_op jit(solution)/shard_map/all_to_all | solution.py:89
  874.0 21.5 %all-to-all-start.7 = ((bf16[32,64,1024]{2,1,0:T(8,128)(2,1)}), bf16[32,64,1024]{2,1,0:T(8,128)(2,1)}, u32[]{:S(2)}, u32[]{:S(2)}) async-start(bf16[32,64,1024]{2,1,0:T(8,128)(2,1)} %bitcast.87), calls=%async_computation.7 | async-start | bytes 8388608 | tf_op jit(solution)/shard_map/all_to_all | solution.py:92
  895.8 67.4 %scatter_custom_fusion.1 = f32[4096,1024]{1,0:T(8,128)} fusion(f32[4096,1024]{1,0:T(8,128)} %scatter_custom_fusion, s32[6656]{0:T(1024)S(1)} %fusion.66, bf16[6656,1024]{1,0:T(8,128)(2,1)} %bitcast.28), kind=kCustom, calls=%fused_computation.35 | custom fusion | flops 13631488 | bytes 30408704 | tf_op jit(solution)/shard_map/scatter-add | solution.py:85
  963.2 6.3 all-to-all-start.8
  969.7 29.6 %scatter_custom_fusion.2 = f32[4096,1024]{1,0:T(8,128)} fusion(f32[4096,1024]{1,0:T(8,128)} %scatter_custom_fusion.1, s32[2048]{0:T(1024)S(1)} %bitcast.102, bf16[2048,1024]{1,0:T(8,128)(2,1)} %bitcast.29), kind=kCustom, calls=%fused_computation.50 | custom fusion | flops 4194304 | bytes 20971520 | tf_op jit(solution)/shard_map/scatter-add | solution.py:85
  999.2 20.7 %scatter_custom_fusion.3 = f32[4096,1024]{1,0:T(8,128)} fusion(f32[4096,1024]{1,0:T(8,128)} %scatter_custom_fusion.2, s32[1024]{0:T(1024)S(1)} %bitcast.103, bf16[1024,1024]{1,0:T(8,128)(2,1)S(1)} %bitcast.86), kind=kCustom, calls=%fused_computation.67 | custom fusion | flops 2097152 | bytes 18874368 | tf_op jit(solution)/shard_map/scatter-add | solution.py:85
  1020.0 9.1 convert_element_type.77
  (65 shorter events, 17.3 us)
Async XLA Ops:
  42.6 31.1 %all-to-all-start.1 = ((bf16[32,32,1024]{2,1,0:T(8,128)(2,1)}), bf16[32,32,1024]{2,1,0:T(8,128)(2,1)S(1)}, u32[]{:S(2)}, u32[]{:S(2)}) async-start(bf16[32,32,1024]{2,1,0:T(8,128)(2,1)} %bitcast.9), calls=%async_computation.1 | async-start | bytes 4194304 | tf_op jit(solution)/shard_map/all_to_all | solution.py:73
  73.7 40.7 %copy-start = (bf16[32,32,1024]{2,1,0:T(8,128)(2,1)}, bf16[32,32,1024]{2,1,0:T(8,128)(2,1)S(1)}, u32[]{:S(2)}) copy-start(bf16[32,32,1024]{2,1,0:T(8,128)(2,1)S(1)} %all-to-all-done.1) | copy-start | bytes 6291460
  73.7 57.3 %all-to-all-start.2 = ((bf16[32,64,1024]{2,1,0:T(8,128)(2,1)}), bf16[32,64,1024]{2,1,0:T(8,128)(2,1)}, u32[]{:S(2)}, u32[]{:S(2)}) async-start(bf16[32,64,1024]{2,1,0:T(8,128)(2,1)} %bitcast.83), calls=%async_computation.2 | async-start | bytes 8388608 | tf_op jit(solution)/shard_map/all_to_all | solution.py:73
  131.0 177.7 %all-to-all-start.3 = ((bf16[32,208,1024]{2,1,0:T(8,128)(2,1)}), bf16[32,208,1024]{2,1,0:T(8,128)(2,1)}, u32[]{:S(2)}, u32[]{:S(2)}) async-start(bf16[32,208,1024]{2,1,0:T(8,128)(2,1)} %bitcast.81), calls=%async_computation.3 | async-start | bytes 27262976 | tf_op jit(solution)/shard_map/all_to_all | solution.py:73
  141.1 11.3 %copy-start.5 = (f32[32,4,128]{2,1,0:T(4,128)S(1)}, f32[32,4,128]{2,1,0:T(4,128)}, u32[]{:S(2)}) copy-start(f32[32,4,128]{2,1,0:T(4,128)} %get-tuple-element.26) | copy-start | bytes 196612
  308.7 186.8 %all-to-all-start.5 = ((bf16[32,208,1024]{2,1,0:T(8,128)(2,1)}), bf16[32,208,1024]{2,1,0:T(8,128)(2,1)}, u32[]{:S(2)}, u32[]{:S(2)}) async-start(bf16[32,208,1024]{2,1,0:T(8,128)(2,1)} %bitcast.82), calls=%async_computation.5 | async-start | bytes 27262976 | tf_op jit(solution)/shard_map/all_to_all | solution.py:73
  327.6 84.2 %copy-start.7 = (f32[6656]{0:T(1024)S(1)}, f32[6656]{0:T(1024)}, u32[]{:S(2)}) copy-start(f32[6656]{0:T(1024)} %mul.140) | copy-start | bytes 79876
  495.5 189.3 %all-to-all-start.4 = ((bf16[32,208,1024]{2,1,0:T(8,128)(2,1)}), bf16[32,208,1024]{2,1,0:T(8,128)(2,1)}, u32[]{:S(2)}, u32[]{:S(2)}) async-start(bf16[32,208,1024]{2,1,0:T(8,128)(2,1)} %bitcast.85), calls=%async_computation.4 | async-start | bytes 27262976 | tf_op jit(solution)/shard_map/all_to_all | solution.py:88
  516.9 84.4 %copy-start.6 = (f32[6656]{0:T(1024)S(1)}, f32[6656]{0:T(1024)}, u32[]{:S(2)}) copy-start(f32[6656]{0:T(1024)} %mul.147) | copy-start | bytes 79876
  665.8 40.4 %copy-start.1 = (bf16[32,32,1024]{2,1,0:T(8,128)(2,1)S(1)}, bf16[32,32,1024]{2,1,0:T(8,128)(2,1)}, u32[]{:S(2)}) copy-start(bf16[32,32,1024]{2,1,0:T(8,128)(2,1)} %copy-done) | copy-start | bytes 6291460
  665.8 40.4 %copy-start.9 = (f32[1024]{0:T(1024)S(1)}, f32[1024]{0:T(1024)}, u32[]{:S(2)}) copy-start(f32[1024]{0:T(1024)} %mul.130) | copy-start | bytes 12292
  684.7 189.3 %all-to-all-start.6 = ((bf16[32,208,1024]{2,1,0:T(8,128)(2,1)}), bf16[32,208,1024]{2,1,0:T(8,128)(2,1)}, u32[]{:S(2)}, u32[]{:S(2)}) async-start(bf16[32,208,1024]{2,1,0:T(8,128)(2,1)} %bitcast.84), calls=%async_computation.6 | async-start | bytes 27262976 | tf_op jit(solution)/shard_map/all_to_all | solution.py:89
  731.1 30.6 %copy-start.8 = (f32[2048]{0:T(1024)S(1)}, f32[2048]{0:T(1024)}, u32[]{:S(2)}) copy-start(f32[2048]{0:T(1024)} %mul.120) | copy-start | bytes 24580
  731.1 30.6 %copy-start.10 = (bf16[1,4096,1024]{2,1,0:T(8,128)(2,1)S(1)}, bf16[1,4096,1024]{2,1,0:T(8,128)(2,1)}, u32[]{:S(2)}) copy-start(bf16[1,4096,1024]{2,1,0:T(8,128)(2,1)} %param.9) | copy-start | bytes 25165828
  782.9 112.6 %copy-start.2 = (s32[32,208]{1,0:T(8,128)S(1)}, s32[32,208]{1,0:T(8,128)}, u32[]{:S(2)}) copy-start(s32[32,208]{1,0:T(8,128)} %get-tuple-element.45) | copy-start | bytes 79876
  874.0 89.1 %all-to-all-start.7 = ((bf16[32,64,1024]{2,1,0:T(8,128)(2,1)}), bf16[32,64,1024]{2,1,0:T(8,128)(2,1)}, u32[]{:S(2)}, u32[]{:S(2)}) async-start(bf16[32,64,1024]{2,1,0:T(8,128)(2,1)} %bitcast.87), calls=%async_computation.7 | async-start | bytes 8388608 | tf_op jit(solution)/shard_map/all_to_all | solution.py:92
  895.8 73.7 %copy-start.4 = (s32[32,64]{1,0:T(8,128)S(1)}, s32[32,64]{1,0:T(8,128)}, u32[]{:S(2)}) copy-start(s32[32,64]{1,0:T(8,128)} %get-tuple-element.43) | copy-start | bytes 24580
  895.8 73.8 %copy-start.3 = (s32[32,32]{1,0:T(8,128)S(1)}, s32[32,32]{1,0:T(8,128)}, u32[]{:S(2)}) copy-start(s32[32,32]{1,0:T(8,128)} %get-tuple-element.41) | copy-start | bytes 12292
  963.2 36.1 %all-to-all-start.8 = ((bf16[32,32,1024]{2,1,0:T(8,128)(2,1)}), bf16[32,32,1024]{2,1,0:T(8,128)(2,1)S(1)}, u32[]{:S(2)}, u32[]{:S(2)}) async-start(bf16[32,32,1024]{2,1,0:T(8,128)(2,1)} %bitcast.89), calls=%async_computation.8 | async-start | bytes 4194304 | tf_op jit(solution)/shard_map/all_to_all | solution.py:95

commit v3 on v1

--- a/solution.py
+++ b/solution.py
@@ -62,7 +62,7 @@
         request = jnp.where(lane[None] < counts[:, None], wsel.reshape(group_n, pair_cap) - bounds[:-1, None], -1)
         wgate = wgate.reshape(group_n, pair_cap)
         asked = lax.all_to_all(request, "ep", 0, 0, tiled=True)
-        cuts = (0, pair_cap // 8, pair_cap * 9 // 16, pair_cap)
+        cuts = (0, pair_cap * 5 // 32, pair_cap * 37 // 64, pair_cap)
         parts = [slice(cuts[i], cuts[i + 1]) for i in range(3)]
         got = []
         for part in parts:

time: 1040 us -> 1030 us (level); the launches traced: 1030 us -> 1030 us
  starting transfers between devices: 102 us -> 117 us
  waiting for transfers between devices: 236 us -> 222 us
    all_to_all x1, waiting for transfers between devices: 45 us -> 25.8 us  [local_layer(): back2 = lax.all_to_all(weighted[2], 'ep', 0, 0, tiled=True)]
    all_to_all x1, starting transfers between devices: 19.5 us -> 31.4 us  [local_layer(): back1 = lax.all_to_all(weighted[1], 'ep', 0, 0, tiled=True)]
  transfers between devices with their start and end apart: 6 -> 6, of which waited for: 5 -> 5; matrix products, arithmetic and copies ran while one was open for 59% -> 58% of each run, Pallas kernels for 0% -> 0%
where the time goes in v3:
time: 1030 us
  matrix products  371 us (36%)
  waiting for transfers between devices  222 us (22%)
  other arithmetic  209 us (20%)
  starting transfers between devices  117 us (11%)
  local copies, waits for them, and re-layouts  91 us (9%)
  blocking collectives  16.1 us (2%)
    dot_general x3, matrix products, local_layer(): jnp.dot(x.reshape(-1, model_dim), win_loc[0], preferred_element_type=jnp....  210 us
    scatter-add x3, other arithmetic, add_rows(): acc.at[at].add(rows.reshape(-1, model_dim).astype(jnp.float32), mode='drop')  178 us
    all_to_all x3, waiting for transfers between devices, local_layer(): got.append(lax.all_to_all(rows, 'ep', 0, 0, tiled=True))  176 us
    dot_general x3, matrix products, local_layer(): o = jnp.dot(hidden, wout_loc[0], preferred_element_type=jnp.float32)  161 us
    gather x3, local copies, waits for them, and re-layouts, local_layer(): rows = tok_loc[idx].reshape(group_n, part.stop - part.start, model_dim)  86.2 us
    all_to_all x3, starting transfers between devices, local_layer(): got.append(lax.all_to_all(rows, 'ep', 0, 0, tiled=True))  41.7 us
    all_to_all x1, starting transfers between devices, local_layer(): back1 = lax.all_to_all(weighted[1], 'ep', 0, 0, tiled=True)  31.4 us
    all_to_all x1, waiting for transfers between devices, local_layer(): back2 = lax.all_to_all(weighted[2], 'ep', 0, 0, tiled=True)  25.8 us
  transfers between devices with their start and end apart: 6, of which 5 were waited for; matrix products, arithmetic and copies ran while one was open for 58% of the time, Pallas kernels for 0%

profile of v3, /device:TPU:97, one launch (start us, length us, event | category | flops | bytes accessed | tf_op | source)
XLA Modules:
  0.0 1032.3 jit_solution(4508946838850331822)
XLA Ops:
  0.0 7.7 sort.23
  9.8 4.5 shard_map.55
  14.3 1.0 compare_select_fusion
  15.3 16.1 %all_to_all.39 = s32[32,1,512]{2,1,0:T(1,128)S(1)} all-to-all(s32[32,1,512]{2,1,0:T(1,128)S(1)} %compare_select_fusion), channel_id=1, replica_groups=mesh['dp'=1,'ep'=32] {'ep'}, dimensions={0} | all-to-all | bytes 131072 | tf_op jit(solution)/shard_map/all_to_all | solution.py:64
  32.1 16.5 %gather_fusion = bf16[2560,1024]{1,0:T(8,128)(2,1)} fusion(bf16[4096,1024]{1,0:T(8,128)(2,1)} %param.5, s32[3072]{0:T(1024)S(1)} %pad_clamp_fusion.2), kind=kCustom, calls=%fused_computation | custom fusion | bytes 10496000 | tf_op jit(solution)/shard_map/gather | solution.py:70
  48.7 3.8 all-to-all-start.1
  53.4 34.9 %gather_fusion.1 = bf16[6912,1024]{1,0:T(8,128)(2,1)} fusion(bf16[4096,1024]{1,0:T(8,128)(2,1)} %param.5, s32[7168]{0:T(1024)S(1)} %pad_clamp_fusion.1), kind=kCustom, calls=%fused_computation.1 | custom fusion | bytes 28339200 | tf_op jit(solution)/shard_map/gather | solution.py:70
  88.2 28.5 %all-to-all-done.1 = bf16[32,80,1024]{2,1,0:T(8,128)(2,1)} async-done(((bf16[32,80,1024]{2,1,0:T(8,128)(2,1)}), bf16[32,80,1024]{2,1,0:T(8,128)(2,1)}, u32[]{:S(2)}, u32[]{:S(2)}) %all-to-all-start.1) | async-done | bytes 5242912 | tf_op jit(solution)/shard_map/all_to_all | solution.py:71
  116.7 20.1 %all-to-all-start.2 = ((bf16[32,216,1024]{2,1,0:T(8,128)(2,1)}), bf16[32,216,1024]{2,1,0:T(8,128)(2,1)}, u32[]{:S(2)}, u32[]{:S(2)}) async-start(bf16[32,216,1024]{2,1,0:T(8,128)(2,1)} %bitcast.61), calls=%async_computation.2 | async-start | bytes 28311552 | tf_op jit(solution)/shard_map/all_to_all | solution.py:71
  137.6 0.7 mul.99
  138.3 0.7 mul.106
  139.2 34.8 %gather_fusion.2 = bf16[6912,1024]{1,0:T(8,128)(2,1)} fusion(bf16[4096,1024]{1,0:T(8,128)(2,1)} %param.5, s32[7168]{0:T(1024)S(1)} %pad_clamp_fusion), kind=kCustom, calls=%fused_computation.2 | custom fusion | bytes 28339200 | tf_op jit(solution)/shard_map/gather | solution.py:70
  174.1 136.8 %all-to-all-done.2 = bf16[32,216,1024]{2,1,0:T(8,128)(2,1)} async-done(((bf16[32,216,1024]{2,1,0:T(8,128)(2,1)}), bf16[32,216,1024]{2,1,0:T(8,128)(2,1)}, u32[]{:S(2)}, u32[]{:S(2)}) %all-to-all-start.2) | async-done | bytes 14155808 | tf_op jit(solution)/shard_map/all_to_all | solution.py:71
  310.8 17.8 %all-to-all-start.4 = ((bf16[32,216,1024]{2,1,0:T(8,128)(2,1)}), bf16[32,216,1024]{2,1,0:T(8,128)(2,1)}, u32[]{:S(2)}, u32[]{:S(2)}) async-start(bf16[32,216,1024]{2,1,0:T(8,128)(2,1)} %bitcast.62), calls=%async_computation.4 | async-start | bytes 28311552 | tf_op jit(solution)/shard_map/all_to_all | solution.py:71
  328.7 87.4 %fusion.7 = bf16[6912,4096]{1,0:T(8,128)(2,1)} fusion(bf16[6912,1024]{1,0:T(8,128)(2,1)} %bitcast.11, bf16[1,1024,4096]{2,1,0:T(8,128)(2,1)} %param.8), kind=kOutput, calls=%fused_computation.15 | convolution fusion | flops 58236862464 | bytes 79167488 | tf_op jit(solution)/shard_map/dot_general | solution.py:74
  416.1 66.4 %multiply_convert_fusion.1 = bf16[6912,1024]{1,0:T(8,128)(2,1)} fusion(bf16[6912,4096]{1,0:T(8,128)(2,1)} %fusion.7, f32[6912]{0:T(1024)S(1)} %copy-done.6, bf16[1,4096,1024]{2,1,0:T(8,128)(2,1)} %param.9), kind=kOutput, calls=%fused_computation.38 | convolution fusion | flops 57996214272 | bytes 79195136 | tf_op jit(solution)/shard_map/dot_general | solution.py:76
  482.4 10.8 %all-to-all-done.4 = bf16[32,216,1024]{2,1,0:T(8,128)(2,1)} async-done(((bf16[32,216,1024]{2,1,0:T(8,128)(2,1)}), bf16[32,216,1024]{2,1,0:T(8,128)(2,1)}, u32[]{:S(2)}, u32[]{:S(2)}) %all-to-all-start.4) | async-done | bytes 14155808 | tf_op jit(solution)/shard_map/all_to_all | solution.py:71
  493.2 31.4 %all-to-all-start.3 = ((bf16[32,216,1024]{2,1,0:T(8,128)(2,1)}), bf16[32,216,1024]{2,1,0:T(8,128)(2,1)}, u32[]{:S(2)}, u32[]{:S(2)}) async-start(bf16[32,216,1024]{2,1,0:T(8,128)(2,1)} %bitcast.65), calls=%async_computation.3 | async-start | bytes 28311552 | tf_op jit(solution)/shard_map/all_to_all | solution.py:86
  524.7 87.1 %fusion.15 = bf16[6912,4096]{1,0:T(8,128)(2,1)} fusion(bf16[6912,1024]{1,0:T(8,128)(2,1)} %bitcast.15, bf16[1,1024,4096]{2,1,0:T(8,128)(2,1)} %param.8), kind=kOutput, calls=%fused_computation.23 | convolution fusion | flops 58236862464 | bytes 79167488 | tf_op jit(solution)/shard_map/dot_general | solution.py:74
  611.8 66.4 %multiply_convert_fusion = bf16[6912,1024]{1,0:T(8,128)(2,1)} fusion(bf16[6912,4096]{1,0:T(8,128)(2,1)} %fusion.15, f32[6912]{0:T(1024)S(1)} %copy-done.5, bf16[1,4096,1024]{2,1,0:T(8,128)(2,1)} %param.9), kind=kOutput, calls=%fused_computation.37 | convolution fusion | flops 57996214272 | bytes 79195136 | tf_op jit(solution)/shard_map/dot_general | solution.py:76
  678.2 20.5 %all-to-all-done.3 = bf16[32,216,1024]{2,1,0:T(8,128)(2,1)} async-done(((bf16[32,216,1024]{2,1,0:T(8,128)(2,1)}), bf16[32,216,1024]{2,1,0:T(8,128)(2,1)}, u32[]{:S(2)}, u32[]{:S(2)}) %all-to-all-start.3) | async-done | bytes 14155808 | tf_op jit(solution)/shard_map/all_to_all | solution.py:86
  698.7 21.9 %all-to-all-start.5 = ((bf16[32,216,1024]{2,1,0:T(8,128)(2,1)}), bf16[32,216,1024]{2,1,0:T(8,128)(2,1)}, u32[]{:S(2)}, u32[]{:S(2)}) async-start(bf16[32,216,1024]{2,1,0:T(8,128)(2,1)} %bitcast.64), calls=%async_computation.5 | async-start | bytes 28311552 | tf_op jit(solution)/shard_map/all_to_all | solution.py:87
  720.7 11.4 %convert_element_type.50 = f32[4096,1024]{1,0:T(8,128)} convert(bf16[4096,1024]{1,0:T(8,128)(2,1)} %param.5) | non-fusion elementwise | flops 4194304 | bytes 25165824 | tf_op jit(solution)/shard_map/convert_element_type | solution.py:85
  732.0 0.7 slice.46
  733.1 35.6 %fusion.23.clone.4 = bf16[2560,4096]{1,0:T(8,128)(2,1)} fusion(bf16[2560,1024]{1,0:T(8,128)(2,1)} %bitcast.6, bf16[1,1024,4096]{2,1,0:T(8,128)(2,1)} %param.8), kind=kOutput, calls=%fused_computation.32.clone.clone.clone.1 | convolution fusion | flops 21569208320 | bytes 34603008 | tf_op jit(solution)/shard_map/dot_general | solution.py:74
  768.6 28.5 %multiply_convert_fusion.2 = bf16[2560,1024]{1,0:T(8,128)(2,1)} fusion(bf16[1,4096,1024]{2,1,0:T(8,128)(2,1)} %param.9, f32[2560]{0:T(1024)S(1)} %mul.89, bf16[2560,4096]{1,0:T(8,128)(2,1)} %fusion.23.clone.4), kind=kOutput, calls=%fused_computation.41 | convolution fusion | flops 21480079360 | bytes 34613248 | tf_op jit(solution)/shard_map/dot_general | solution.py:76
  797.2 71.7 %scatter_custom_fusion = f32[4096,1024]{1,0:T(8,128)} fusion(f32[4096,1024]{1,0:T(8,128)} %convert_element_type.50, s32[6912]{0:T(1024)S(1)} %fusion.41, bf16[6912,1024]{1,0:T(8,128)(2,1)} %bitcast.19), kind=kCustom, calls=%fused_computation.35 | custom fusion | flops 14155776 | bytes 30932992 | tf_op jit(solution)/shard_map/scatter-add | solution.py:83
  868.9 25.8 %all-to-all-done.5 = bf16[32,216,1024]{2,1,0:T(8,128)(2,1)} async-done(((bf16[32,216,1024]{2,1,0:T(8,128)(2,1)}), bf16[32,216,1024]{2,1,0:T(8,128)(2,1)}, u32[]{:S(2)}, u32[]{:S(2)}) %all-to-all-start.5) | async-done | bytes 14155808 | tf_op jit(solution)/shard_map/all_to_all | solution.py:87
  894.7 21.9 %all-to-all-start.6 = ((bf16[32,80,1024]{2,1,0:T(8,128)(2,1)}), bf16[32,80,1024]{2,1,0:T(8,128)(2,1)}, u32[]{:S(2)}, u32[]{:S(2)}) async-start(bf16[32,80,1024]{2,1,0:T(8,128)(2,1)} %bitcast.66), calls=%async_computation.6 | async-start | bytes 10485760 | tf_op jit(solution)/shard_map/all_to_all | solution.py:90
  917.0 71.7 %scatter_custom_fusion.1 = f32[4096,1024]{1,0:T(8,128)} fusion(f32[4096,1024]{1,0:T(8,128)} %scatter_custom_fusion, s32[6912]{0:T(1024)S(1)} %fusion.44, bf16[6912,1024]{1,0:T(8,128)(2,1)} %bitcast.20), kind=kCustom, calls=%fused_computation.33 | custom fusion | flops 14155776 | bytes 30932992 | tf_op jit(solution)/shard_map/scatter-add | solution.py:83
  988.8 34.1 %scatter_custom_fusion.2 = f32[4096,1024]{1,0:T(8,128)} fusion(f32[4096,1024]{1,0:T(8,128)} %scatter_custom_fusion.1, s32[2560]{0:T(1024)S(1)} %fusion.46, bf16[2560,1024]{1,0:T(8,128)(2,1)} %bitcast.21), kind=kCustom, calls=%fused_computation.39 | custom fusion | flops 5242880 | bytes 22020096 | tf_op jit(solution)/shard_map/scatter-add | solution.py:83
  1022.8 9.1 convert_element_type.61
  (42 shorter events, 5.3 us)
Async XLA Ops:
  48.7 68.1 %all-to-all-start.1 = ((bf16[32,80,1024]{2,1,0:T(8,128)(2,1)}), bf16[32,80,1024]{2,1,0:T(8,128)(2,1)}, u32[]{:S(2)}, u32[]{:S(2)}) async-start(bf16[32,80,1024]{2,1,0:T(8,128)(2,1)} %bitcast.63), calls=%async_computation.1 | async-start | bytes 10485760 | tf_op jit(solution)/shard_map/all_to_all | solution.py:71
  88.2 48.6 %copy-start.4 = (f32[32,4,128]{2,1,0:T(4,128)S(1)}, f32[32,4,128]{2,1,0:T(4,128)}, u32[]{:S(2)}) copy-start(f32[32,4,128]{2,1,0:T(4,128)} %get-tuple-element.16) | copy-start | bytes 196612
  116.7 194.1 %all-to-all-start.2 = ((bf16[32,216,1024]{2,1,0:T(8,128)(2,1)}), bf16[32,216,1024]{2,1,0:T(8,128)(2,1)}, u32[]{:S(2)}, u32[]{:S(2)}) async-start(bf16[32,216,1024]{2,1,0:T(8,128)(2,1)} %bitcast.61), calls=%async_computation.2 | async-start | bytes 28311552 | tf_op jit(solution)/shard_map/all_to_all | solution.py:71
  136.9 0.6 copy-start
  310.8 182.4 %all-to-all-start.4 = ((bf16[32,216,1024]{2,1,0:T(8,128)(2,1)}), bf16[32,216,1024]{2,1,0:T(8,128)(2,1)}, u32[]{:S(2)}, u32[]{:S(2)}) async-start(bf16[32,216,1024]{2,1,0:T(8,128)(2,1)} %bitcast.62), calls=%async_computation.4 | async-start | bytes 28311552 | tf_op jit(solution)/shard_map/all_to_all | solution.py:71
  328.7 87.4 %copy-start.6 = (f32[6912]{0:T(1024)S(1)}, f32[6912]{0:T(1024)}, u32[]{:S(2)}) copy-start(f32[6912]{0:T(1024)} %mul.99) | copy-start | bytes 82948
  493.2 205.5 %all-to-all-start.3 = ((bf16[32,216,1024]{2,1,0:T(8,128)(2,1)}), bf16[32,216,1024]{2,1,0:T(8,128)(2,1)}, u32[]{:S(2)}, u32[]{:S(2)}) async-start(bf16[32,216,1024]{2,1,0:T(8,128)(2,1)} %bitcast.65), calls=%async_computation.3 | async-start | bytes 28311552 | tf_op jit(solution)/shard_map/all_to_all | solution.py:86
  524.6 87.2 %copy-start.5 = (f32[6912]{0:T(1024)S(1)}, f32[6912]{0:T(1024)}, u32[]{:S(2)}) copy-start(f32[6912]{0:T(1024)} %mul.106) | copy-start | bytes 82948
  698.7 196.0 %all-to-all-start.5 = ((bf16[32,216,1024]{2,1,0:T(8,128)(2,1)}), bf16[32,216,1024]{2,1,0:T(8,128)(2,1)}, u32[]{:S(2)}, u32[]{:S(2)}) async-start(bf16[32,216,1024]{2,1,0:T(8,128)(2,1)} %bitcast.64), calls=%async_computation.5 | async-start | bytes 28311552 | tf_op jit(solution)/shard_map/all_to_all | solution.py:87
  720.6 12.2 %copy-start.2 = (s32[32,216]{1,0:T(8,128)S(1)}, s32[32,216]{1,0:T(8,128)}, u32[]{:S(2)}) copy-start(s32[32,216]{1,0:T(8,128)} %get-tuple-element.26) | copy-start | bytes 82948
  797.2 119.5 %copy-start.1 = (s32[32,216]{1,0:T(8,128)S(1)}, s32[32,216]{1,0:T(8,128)}, u32[]{:S(2)}) copy-start(s32[32,216]{1,0:T(8,128)} %get-tuple-element.23) | copy-start | bytes 82948
  797.2 119.6 %copy-start.3 = (s32[32,80]{1,0:T(8,128)S(1)}, s32[32,80]{1,0:T(8,128)}, u32[]{:S(2)}) copy-start(s32[32,80]{1,0:T(8,128)} %get-tuple-element.21) | copy-start | bytes 30724
  894.7 94.1 %all-to-all-start.6 = ((bf16[32,80,1024]{2,1,0:T(8,128)(2,1)}), bf16[32,80,1024]{2,1,0:T(8,128)(2,1)}, u32[]{:S(2)}, u32[]{:S(2)}) async-start(bf16[32,80,1024]{2,1,0:T(8,128)(2,1)} %bitcast.66), calls=%async_computation.6 | async-start | bytes 10485760 | tf_op jit(solution)/shard_map/all_to_all | solution.py:90
